TPU v7x, 32 devices: a whole 2x2x4 slice. The times are simulated.
32 devices in a mesh: ctx: 8 (over z, y), head: 4 (over x, core).
Axes of the slice: x: 2, y: 2, z: 4, core: 2. Of those that a mesh axis runs over, the one named last changes fastest.
Arguments:
- hidden: bfloat16 [1024, 4096], P('ctx', 'head'), may hold values from -6 to 6
- w_proj: bfloat16 [4096, 1024], P('head'), may hold values from -0.125 to 0.125
- b_proj: bfloat16 [4096, 8], P('head'), may hold values from -0.09375 to 0.09375
- queries: bfloat16 [1024, 4096], P('ctx', 'head'), may hold values from -300 to 300
- keys: bfloat16 [1024, 1024], P('ctx', 'head'), may hold values from -6 to 6
- values: bfloat16 [1024, 1024], P('ctx', 'head'), may hold values from -6 to 6
- reach: int32 [8], P('ctx'), may hold values from 1 to 5
Outputs:
- numer: float32 [1024, 4096], P('ctx', 'head')
- totals: float32 [32, 1024], P('head', 'ctx')
- maxima: float32 [32, 1024], P('head', 'ctx')
- carried: bfloat16 [1024, 4096], P('ctx', 'head')
All inputs are finite; a program needn't handle non-finite values.
Results may differ from a plain program's by a relative error of at most 0.0064.
Values may be sent and summed in bfloat16 or wider, within the bound.
A program may use at most 64 MiB of HBM per device.

v0:
```python
import jax
import jax.numpy as jnp
from jax import lax
from jax.sharding import PartitionSpec as P

STEPS = 5


very_low = -1e30
highest = lax.Precision.HIGHEST


def passed_along(array, axis, by):
    length = lax.axis_size(axis)
    pairs = [(i, i + by) for i in range(length) if 0 <= i + by < length]
    return lax.ppermute(array, axis, pairs)


def transitions(raw_dirs, logits):
    vectors = raw_dirs * lax.rsqrt(jnp.sum(raw_dirs * raw_dirs, axis=-1, keepdims=True) + 1e-06)
    beta_vals = 2.0 / (1.0 + jnp.exp(-logits))
    gram_mat = jnp.einsum("hte,hue->htu", vectors, vectors, precision=highest)
    length = vectors.shape[1]
    identity = jnp.eye(length, dtype=vectors.dtype)
    lower_mat = identity[None] + beta_vals[:, :, None] * jnp.tril(gram_mat, -1)
    diag_beta = identity[None] * beta_vals[:, None, :]
    triangle = lax.linalg.triangular_solve(
        lower_mat, diag_beta, left_side=True, lower=True, unit_diagonal=True
    )
    return (vectors, triangle)


def key_terms(vectors, triangle, key_float):
    key_tri = jnp.triu(jnp.einsum("hue,hje->huj", vectors, key_float, precision=highest), 1)
    key_mix = jnp.einsum("htu,huj->htj", triangle, key_tri, precision=highest)
    keys_moved = (
        key_float - jnp.einsum("htj,hte->hje", key_mix, vectors, precision=highest)
    ).astype(jnp.bfloat16)
    identity = jnp.eye(vectors.shape[2], dtype=vectors.dtype)
    block_prod = identity[None] - jnp.einsum(
        "hte,htu,huf->hef", vectors, triangle, vectors, precision=highest
    )
    return (keys_moved, block_prod, key_tri)


def query_terms(vectors, triangle, query_float):
    query_vec = jnp.tril(jnp.einsum("hgie,hte->hgit", query_float, vectors, precision=highest))
    query_tri = jnp.einsum("hgit,htu->hgiu", query_vec, triangle, precision=highest)
    query_hat = query_float - jnp.einsum("hgiu,hue->hgie", query_tri, vectors, precision=highest)
    return (query_hat, query_tri)


def body(hidden, w_proj, b_proj, queries, keys, values, reach):
    length = hidden.shape[0]
    all_heads = b_proj.shape[1]
    head_dim = w_proj.shape[1] // all_heads
    scaling = head_dim ** (-0.5)
    term_dirs = jnp.einsum(
        "ld,dhe->hle",
        hidden,
        w_proj.reshape(w_proj.shape[0], all_heads, head_dim),
        preferred_element_type=jnp.float32,
    )
    term_logit = jnp.einsum("ld,dh->hl", hidden, b_proj, preferred_element_type=jnp.float32)
    raw_dirs, logits = (
        lax.psum_scatter(term_dirs, "head", scatter_dimension=0, tiled=True),
        lax.psum_scatter(term_logit, "head", scatter_dimension=0, tiled=True),
    )
    kv_heads = raw_dirs.shape[0]
    groups = queries.shape[1] // (kv_heads * head_dim)
    key_heads = keys.reshape(length, kv_heads, head_dim).transpose(1, 0, 2)
    value_heads = values.reshape(length, kv_heads, head_dim).transpose(1, 0, 2)
    query_heads = queries.reshape(length, kv_heads, groups, head_dim).transpose(1, 2, 0, 3)
    vectors, triangle = transitions(raw_dirs, logits)
    keys_moved, block_prod, key_tri = key_terms(vectors, triangle, key_heads.astype(jnp.float32))
    query_hat, query_tri = query_terms(vectors, triangle, query_heads.astype(jnp.float32))
    own = jnp.einsum("hgie,hje->hgij", query_heads, key_heads, preferred_element_type=jnp.float32)
    own = own - jnp.einsum("hgiu,huj->hgij", query_tri, key_tri, precision=highest)
    causal = jnp.arange(length)[:, None] >= jnp.arange(length)[None, :]
    own = jnp.where(causal, own * scaling, very_low)
    maxima = jnp.max(own, axis=-1)
    probs = jnp.exp(own - maxima[..., None])
    totals = jnp.sum(probs, axis=-1)
    numer_acc = jnp.einsum(
        "hgij,hje->hgie",
        probs.astype(jnp.bfloat16),
        value_heads,
        preferred_element_type=jnp.float32,
    )
    ctx_index = lax.axis_index("ctx")
    reach_now = reach[0]
    identity = jnp.eye(head_dim, dtype=jnp.float32)
    state = (maxima, totals, numer_acc, query_hat)
    passing_kv = (keys_moved, value_heads)
    passing_prod = block_prod
    for offset in range(1, STEPS):
        passing_kv = passed_along((passing_kv[0], passing_kv[1]), "ctx", 1)
        passing_prod = passed_along(passing_prod, "ctx", 1)
        step_prod = passing_prod
        visit_maxima, visit_totals, visit_numer_acc, visit_carried_q = state
        keys_in, values_in = passing_kv
        source = ctx_index - offset
        is_live = jnp.logical_and(offset < reach_now, source >= 0)
        scores = (
            jnp.einsum(
                "hgie,hje->hgij",
                visit_carried_q.astype(jnp.bfloat16),
                keys_in,
                preferred_element_type=jnp.float32,
            )
            * scaling
        )
        scores = jnp.where(is_live, scores, very_low)
        max_new = jnp.maximum(visit_maxima, jnp.max(scores, axis=-1))
        rescale = jnp.exp(visit_maxima - max_new)
        visit_probs = jnp.exp(scores - max_new[..., None])
        visit_totals = visit_totals * rescale + jnp.sum(visit_probs, axis=-1)
        visit_numer_acc = visit_numer_acc * rescale[..., None] + jnp.einsum(
            "hgij,hje->hgie",
            visit_probs.astype(jnp.bfloat16),
            values_in,
            preferred_element_type=jnp.float32,
        )
        step_prod = jnp.where(source >= 0, step_prod, identity[None])
        visit_carried_q = jnp.einsum(
            "hgie,hef->hgif", visit_carried_q, step_prod, precision=highest
        )
        state = (max_new, visit_totals, visit_numer_acc, visit_carried_q)
    maxima, totals, numer_acc, carried_q = state
    numer = numer_acc.transpose(2, 0, 1, 3).reshape(length, kv_heads * groups * head_dim)
    carried = (
        carried_q.astype(jnp.bfloat16)
        .transpose(2, 0, 1, 3)
        .reshape(length, kv_heads * groups * head_dim)
    )
    return (
        numer,
        totals.reshape(kv_heads * groups, length),
        maxima.reshape(kv_heads * groups, length),
        carried,
    )


def solution(mesh):
    in_specs = (
        P("ctx", "head"),
        P("head", None),
        P("head", None),
        P("ctx", "head"),
        P("ctx", "head"),
        P("ctx", "head"),
        P("ctx"),
    )
    out_specs = (P("ctx", "head"), P("head", "ctx"), P("head", "ctx"), P("ctx", "head"))
    return jax.shard_map(body, mesh=mesh, in_specs=in_specs, out_specs=out_specs, check_vma=False)
```

profile of v0, /device:TPU:8, one launch (start us, length us, event | category | flops | bytes accessed | tf_op | source)
XLA Modules:
  0.0 121.9 jit_solution(7018643259088853638)
XLA Ops:
  7.2 2.9 %copy.118 = bf16[1024,1024]{0,1:T(8,128)(2,1)S(1)} copy(bf16[1024,1024]{1,0:T(8,128)(2,1)} %param.8) | data formatting | bytes 4194304 | tf_op jit(solution)/shard_map/reshape | solution.py:61
  10.2 1.5 %convolution_bitcast_fusion.6 = f32[8,128,128]{1,2,0:T(8,128)} fusion(bf16[1024,8,128]{0,2,1:T(8,128)(2,1)S(1)} %bitcast.247, bf16[128,1024]{1,0:T(8,128)(2,1)S(1)} %copy-done), kind=kOutput, calls=%fused_computation.7 | convolution fusion | flops 268435456 | bytes 2883584 | tf_op jit(solution)/shard_map/ld,dhe->hle/dot_general | solution.py:58
  11.9 3.4 %collective-permute-start.1 = (bf16[2,128,128]{1,2,0:T(8,128)(2,1)S(1)}, bf16[2,128,128]{1,2,0:T(8,128)(2,1)S(1)}, u32[]{:S(2)}, u32[]{:S(2)}) collective-permute-start(bf16[2,128,128]{1,2,0:T(8,128)(2,1)S(1)} %bitcast.251), channel_id=1, source_target_pairs={{0,4},{4,8},{8,12},{12,16},{16,20},{20,24},{24,28},{1,5},{5,9},{9,... | collective-permute-start | bytes 196616 | tf_op jit(solution)/shard_map/ppermute | solution.py:16
  18.3 6.3 %all-reduce = f32[8,128]{1,0:T(8,128)S(1)} all-reduce(f32[8,128]{1,0:T(8,128)S(1)} %fusion.117), channel_id=3, replica_groups=mesh['ctx'=8,'head'=4] {'head'}, use_global_device_ids=true, to_apply=%region_2.0.clone | all-reduce | flops 1024 | bytes 8192
  24.6 3.4 %collective-permute-start.4 = (bf16[2,128,128]{1,2,0:T(8,128)(2,1)S(1)}, bf16[2,128,128]{1,2,0:T(8,128)(2,1)S(1)}, u32[]{:S(2)}, u32[]{:S(2)}) collective-permute-start(bf16[2,128,128]{1,2,0:T(8,128)(2,1)S(1)} %collective-permute-done.1), channel_id=1, source_target_pairs={{0,4},{4,8},{8,12},{12,16},{16,20},{20,24},{24,28},{1,5},{5,9},{9,... | collective-permute-start | bytes 196616 | tf_op jit(solution)/shard_map/ppermute | solution.py:16
  28.1 3.6 %collective-permute-done.4 = bf16[2,128,128]{1,2,0:T(8,128)(2,1)S(1)} collective-permute-done((bf16[2,128,128]{1,2,0:T(8,128)(2,1)S(1)}, bf16[2,128,128]{1,2,0:T(8,128)(2,1)S(1)}, u32[]{:S(2)}, u32[]{:S(2)}) %collective-permute-start.4) | collective-permute-done | bytes 65568 | tf_op jit(solution)/shard_map/ppermute | solution.py:16
  31.7 2.5 %collective-permute-start.7 = (bf16[2,128,128]{1,2,0:T(8,128)(2,1)S(1)}, bf16[2,128,128]{1,2,0:T(8,128)(2,1)S(1)}, u32[]{:S(2)}, u32[]{:S(2)}) collective-permute-start(bf16[2,128,128]{1,2,0:T(8,128)(2,1)S(1)} %collective-permute-done.4), channel_id=1, source_target_pairs={{0,4},{4,8},{8,12},{12,16},{16,20},{20,24},{24,28},{1,5},{5,9},{9,... | collective-permute-start | bytes 196616 | tf_op jit(solution)/shard_map/ppermute | solution.py:16
  34.2 4.5 %collective-permute-done.7 = bf16[2,128,128]{1,2,0:T(8,128)(2,1)S(1)} collective-permute-done((bf16[2,128,128]{1,2,0:T(8,128)(2,1)S(1)}, bf16[2,128,128]{1,2,0:T(8,128)(2,1)S(1)}, u32[]{:S(2)}, u32[]{:S(2)}) %collective-permute-start.7) | collective-permute-done | bytes 65568 | tf_op jit(solution)/shard_map/ppermute | solution.py:16
  38.7 1.9 %collective-permute-start.10 = (bf16[2,128,128]{1,2,0:T(8,128)(2,1)S(1)}, bf16[2,128,128]{1,2,0:T(8,128)(2,1)S(1)}, u32[]{:S(2)}, u32[]{:S(2)}) collective-permute-start(bf16[2,128,128]{1,2,0:T(8,128)(2,1)S(1)} %collective-permute-done.7), channel_id=1, source_target_pairs={{0,4},{4,8},{8,12},{12,16},{16,20},{20,24},{24,28},{1,5},{5,9},{9,... | collective-permute-start | bytes 196616 | tf_op jit(solution)/shard_map/ppermute | solution.py:16
  40.7 1.0 multiply_reduce_fusion
  41.7 1.4 %fusion.19 = f32[2,1,128,128]{3,2,1,0:T(8,128)S(1)} fusion(f32[2,128,128]{1,2,0:T(8,128)} %reduce-scatter.2.cloned.1.call-done, f32[128,128]{1,0:T(8,128)S(1)} %fusion.100, f32[2,128]{1,0:T(2,128)S(1)} %fusion.109, f32[128,128]{1,0:T(8,128)S(1)} %get-tuple-element.40, f32[2,128]{1,0:T(2,128)S(1)} %add_rsqrt_fusion, pred[128,128]{1,0:T(8,128)(4,1)S(1)} %get-tuple-element.39), kind=kOutput, calls=%fused_computation.37 | convolution fusion | flops 50528256 | bytes 411648 | tf_op jit(solution)/shard_map/hte,hue->htu/dot_general | solution.py:22
  43.1 19.7 %custom-call.3 = f32[2,1,128,128]{2,3,1,0:T(8,128)S(1)} custom-call(f32[2,1,128,128]{3,2,1,0:T(8,128)S(1)} %fusion.19), custom_call_target="InvertDiagBlocksLowerTriangular" | custom-call | tf_op jit(solution)/shard_map/triangular_solve | solution.py:27
  63.1 1.2 convolution_select_fusion
  64.7 1.3 %fusion.20 = bf16[2,128,128]{2,1,0:T(8,128)(2,1)S(1)} fusion(f32[2,128,128]{1,2,0:T(8,128)S(1)} %fusion.118, f32[2,128,128]{1,2,0:T(8,128)} %reduce-scatter.2.cloned.1.call-done, bf16[128,2,128]{2,0,1:T(8,128)(2,1)S(1)} %copy.59, f32[2,128]{1,0:T(2,128)S(1)} %add_rsqrt_fusion), kind=kOutput, calls=%fused_computation.38 | convolution fusion | flops 50462720 | bytes 394240 | tf_op jit(solution)/shard_map/htj,hte->hje/dot_general | solution.py:37
  66.0 4.9 %collective-permute-start = (bf16[2,128,128]{2,1,0:T(8,128)(2,1)S(1)}, bf16[2,128,128]{2,1,0:T(8,128)(2,1)S(1)}, u32[]{:S(2)}, u32[]{:S(2)}) collective-permute-start(bf16[2,128,128]{2,1,0:T(8,128)(2,1)S(1)} %fusion.20), channel_id=1, source_target_pairs={{0,4},{4,8},{8,12},{12,16},{16,20},{20,24},{24,28},{1,5},{5,9},{9,... | collective-permute-start | bytes 196616 | tf_op jit(solution)/shard_map/ppermute | solution.py:16
  71.7 1.9 %collective-permute-start.2 = (f32[2,128,128]{2,1,0:T(8,128)S(1)}, f32[2,128,128]{2,1,0:T(8,128)S(1)}, u32[]{:S(2)}, u32[]{:S(2)}) collective-permute-start(f32[2,128,128]{2,1,0:T(8,128)S(1)} %convolution_subtract_fusion.2), channel_id=1, source_target_pairs={{0,4},{4,8},{8,12},{12,16},{16,20},{20,24},{24,28},{1,5},{5,9},{9,... | collective-permute-start | bytes 393224 | tf_op jit(solution)/shard_map/ppermute | solution.py:16
  74.0 1.0 fusion.59
  75.0 0.6 fusion.49
  75.9 0.6 convolution_subtract_fusion.1
  76.6 4.9 %collective-permute-start.3 = (bf16[2,128,128]{2,1,0:T(8,128)(2,1)S(1)}, bf16[2,128,128]{2,1,0:T(8,128)(2,1)S(1)}, u32[]{:S(2)}, u32[]{:S(2)}) collective-permute-start(bf16[2,128,128]{2,1,0:T(8,128)(2,1)S(1)} %collective-permute-done), channel_id=1, source_target_pairs={{0,4},{4,8},{8,12},{12,16},{16,20},{20,24},{24,28},{1,5},{5,9},{9,... | collective-permute-start | bytes 196616 | tf_op jit(solution)/shard_map/ppermute | solution.py:16
  81.8 1.9 %collective-permute-start.5 = (f32[2,128,128]{2,1,0:T(8,128)S(1)}, f32[2,128,128]{2,1,0:T(8,128)S(1)}, u32[]{:S(2)}, u32[]{:S(2)}) collective-permute-start(f32[2,128,128]{2,1,0:T(8,128)S(1)} %collective-permute-done.2), channel_id=1, source_target_pairs={{0,4},{4,8},{8,12},{12,16},{16,20},{20,24},{24,28},{1,5},{5,9},{9,... | collective-permute-start | bytes 393224 | tf_op jit(solution)/shard_map/ppermute | solution.py:16
  84.4 3.9 %collective-permute-start.6 = (bf16[2,128,128]{2,1,0:T(8,128)(2,1)S(1)}, bf16[2,128,128]{2,1,0:T(8,128)(2,1)S(1)}, u32[]{:S(2)}, u32[]{:S(2)}) collective-permute-start(bf16[2,128,128]{2,1,0:T(8,128)(2,1)S(1)} %collective-permute-done.3), channel_id=1, source_target_pairs={{0,4},{4,8},{8,12},{12,16},{16,20},{20,24},{24,28},{1,5},{5,9},{9,... | collective-permute-start | bytes 196616 | tf_op jit(solution)/shard_map/ppermute | solution.py:16
  88.6 2.9 %collective-permute-done.6 = bf16[2,128,128]{2,1,0:T(8,128)(2,1)S(1)} collective-permute-done((bf16[2,128,128]{2,1,0:T(8,128)(2,1)S(1)}, bf16[2,128,128]{2,1,0:T(8,128)(2,1)S(1)}, u32[]{:S(2)}, u32[]{:S(2)}) %collective-permute-start.6) | collective-permute-done | bytes 65568 | tf_op jit(solution)/shard_map/ppermute | solution.py:16
  91.4 3.0 %collective-permute-start.9 = (bf16[2,128,128]{2,1,0:T(8,128)(2,1)S(1)}, bf16[2,128,128]{2,1,0:T(8,128)(2,1)S(1)}, u32[]{:S(2)}, u32[]{:S(2)}) collective-permute-start(bf16[2,128,128]{2,1,0:T(8,128)(2,1)S(1)} %collective-permute-done.6), channel_id=1, source_target_pairs={{0,4},{4,8},{8,12},{12,16},{16,20},{20,24},{24,28},{1,5},{5,9},{9,... | collective-permute-start | bytes 196616 | tf_op jit(solution)/shard_map/ppermute | solution.py:16
  94.5 3.3 %collective-permute-start.8 = (f32[2,128,128]{2,1,0:T(8,128)S(1)}, f32[2,128,128]{2,1,0:T(8,128)S(1)}, u32[]{:S(2)}, u32[]{:S(2)}) collective-permute-start(f32[2,128,128]{2,1,0:T(8,128)S(1)} %collective-permute-done.5), channel_id=1, source_target_pairs={{0,4},{4,8},{8,12},{12,16},{16,20},{20,24},{24,28},{1,5},{5,9},{9,... | collective-permute-start | bytes 393224 | tf_op jit(solution)/shard_map/ppermute | solution.py:16
  98.7 3.6 %collective-permute-done.8 = f32[2,128,128]{2,1,0:T(8,128)S(1)} collective-permute-done((f32[2,128,128]{2,1,0:T(8,128)S(1)}, f32[2,128,128]{2,1,0:T(8,128)S(1)}, u32[]{:S(2)}, u32[]{:S(2)}) %collective-permute-start.8) | collective-permute-done | bytes 131104 | tf_op jit(solution)/shard_map/ppermute | solution.py:16
  104.8 1.0 copy.82
  105.8 2.2 %collective-permute-start.11 = (f32[2,128,128]{2,1,0:T(8,128)S(1)}, f32[2,128,128]{2,1,0:T(8,128)S(1)}, u32[]{:S(2)}, u32[]{:S(2)}) collective-permute-start(f32[2,128,128]{2,1,0:T(8,128)S(1)} %collective-permute-done.8), channel_id=1, source_target_pairs={{0,4},{4,8},{8,12},{12,16},{16,20},{20,24},{24,28},{1,5},{5,9},{9,... | collective-permute-start | bytes 393224 | tf_op jit(solution)/shard_map/ppermute | solution.py:16
  108.0 0.6 multiply_add_fusion
  108.6 4.9 %collective-permute-done.11 = f32[2,128,128]{2,1,0:T(8,128)S(1)} collective-permute-done((f32[2,128,128]{2,1,0:T(8,128)S(1)}, f32[2,128,128]{2,1,0:T(8,128)S(1)}, u32[]{:S(2)}, u32[]{:S(2)}) %collective-permute-start.11) | collective-permute-done | bytes 131104 | tf_op jit(solution)/shard_map/ppermute | solution.py:16
  113.6 0.6 convolution_convert_fusion
  114.2 0.9 copy.83
  (64 shorter events, 8.5 us)
Async XLA Ops:
  7.2 3.0 %copy-start = (bf16[128,1024]{1,0:T(8,128)(2,1)S(1)}, bf16[128,1024]{1,0:T(8,128)(2,1)}, u32[]{:S(2)}) copy-start(bf16[128,1024]{1,0:T(8,128)(2,1)} %param.7) | copy-start | bytes 786436
  7.2 33.5 %reduce-scatter.2.cloned.1.call-start = ((), (), s32[]{:S(2)}) async-start(), calls=%async_computation.1 | async-start | bytes 655360 | tf_op jit(solution)/shard_map/reduce_scatter | solution.py:66
  10.1 1.6 %copy-start.3 = (bf16[128,256]{1,0:T(8,128)(2,1)S(1)}, bf16[128,256]{1,0:T(8,128)(2,1)}, u32[]{:S(2)}) copy-start(bf16[128,256]{1,0:T(8,128)(2,1)} %param.12) | copy-start | bytes 196612
  10.1 5.9 %copy-start.5 = (bf16[1024,8]{0,1:T(8,128)(2,1)S(1)}, bf16[1024,8]{0,1:T(8,128)(2,1)}, u32[]{:S(2)}) copy-start(bf16[1024,8]{0,1:T(8,128)(2,1)} %param.9) | copy-start | bytes 49156
  10.2 6.3 %copy-start.4 = (bf16[128,256]{1,0:T(8,128)(2,1)S(1)}, bf16[128,256]{1,0:T(8,128)(2,1)}, u32[]{:S(2)}) copy-start(bf16[128,256]{1,0:T(8,128)(2,1)} %param.11) | copy-start | bytes 196612
  10.2 6.5 %copy-start.2 = (bf16[128,1024]{1,0:T(8,128)(2,1)S(1)}, bf16[128,1024]{1,0:T(8,128)(2,1)}, u32[]{:S(2)}) copy-start(bf16[128,1024]{1,0:T(8,128)(2,1)} %param.10) | copy-start | bytes 786436
  10.2 6.9 %copy-start.6 = (u32[32]{0:T(128)S(1)}, u32[32]{0:T(128)}, u32[]{:S(2)}) copy-start(u32[32]{0:T(128)} %constant.57) | copy-start | bytes 388
  11.9 12.8 %collective-permute-start.1 = (bf16[2,128,128]{1,2,0:T(8,128)(2,1)S(1)}, bf16[2,128,128]{1,2,0:T(8,128)(2,1)S(1)}, u32[]{:S(2)}, u32[]{:S(2)}) collective-permute-start(bf16[2,128,128]{1,2,0:T(8,128)(2,1)S(1)} %bitcast.251), channel_id=1, source_target_pairs={{0,4},{4,8},{8,12},{12,16},{16,20},{20,24},{24,28},{1,5},{5,9},{9,... | collective-permute-start | bytes 196616 | tf_op jit(solution)/shard_map/ppermute | solution.py:16
  24.6 7.1 %collective-permute-start.4 = (bf16[2,128,128]{1,2,0:T(8,128)(2,1)S(1)}, bf16[2,128,128]{1,2,0:T(8,128)(2,1)S(1)}, u32[]{:S(2)}, u32[]{:S(2)}) collective-permute-start(bf16[2,128,128]{1,2,0:T(8,128)(2,1)S(1)} %collective-permute-done.1), channel_id=1, source_target_pairs={{0,4},{4,8},{8,12},{12,16},{16,20},{20,24},{24,28},{1,5},{5,9},{9,... | collective-permute-start | bytes 196616 | tf_op jit(solution)/shard_map/ppermute | solution.py:16
  31.7 7.0 %collective-permute-start.7 = (bf16[2,128,128]{1,2,0:T(8,128)(2,1)S(1)}, bf16[2,128,128]{1,2,0:T(8,128)(2,1)S(1)}, u32[]{:S(2)}, u32[]{:S(2)}) collective-permute-start(bf16[2,128,128]{1,2,0:T(8,128)(2,1)S(1)} %collective-permute-done.4), channel_id=1, source_target_pairs={{0,4},{4,8},{8,12},{12,16},{16,20},{20,24},{24,28},{1,5},{5,9},{9,... | collective-permute-start | bytes 196616 | tf_op jit(solution)/shard_map/ppermute | solution.py:16
  38.7 65.8 %collective-permute-start.10 = (bf16[2,128,128]{1,2,0:T(8,128)(2,1)S(1)}, bf16[2,128,128]{1,2,0:T(8,128)(2,1)S(1)}, u32[]{:S(2)}, u32[]{:S(2)}) collective-permute-start(bf16[2,128,128]{1,2,0:T(8,128)(2,1)S(1)} %collective-permute-done.7), channel_id=1, source_target_pairs={{0,4},{4,8},{8,12},{12,16},{16,20},{20,24},{24,28},{1,5},{5,9},{9,... | collective-permute-start | bytes 196616 | tf_op jit(solution)/shard_map/ppermute | solution.py:16
  40.7 30.3 %copy-start.1 = (f32[2,128,128]{1,2,0:T(8,128)S(1)}, f32[2,128,128]{1,2,0:T(8,128)}, u32[]{:S(2)}) copy-start(f32[2,128,128]{1,2,0:T(8,128)} %reduce-scatter.2.cloned.1.call-done) | copy-start | bytes 393220
  66.0 10.6 %collective-permute-start = (bf16[2,128,128]{2,1,0:T(8,128)(2,1)S(1)}, bf16[2,128,128]{2,1,0:T(8,128)(2,1)S(1)}, u32[]{:S(2)}, u32[]{:S(2)}) collective-permute-start(bf16[2,128,128]{2,1,0:T(8,128)(2,1)S(1)} %fusion.20), channel_id=1, source_target_pairs={{0,4},{4,8},{8,12},{12,16},{16,20},{20,24},{24,28},{1,5},{5,9},{9,... | collective-permute-start | bytes 196616 | tf_op jit(solution)/shard_map/ppermute | solution.py:16
  71.7 10.2 %collective-permute-start.2 = (f32[2,128,128]{2,1,0:T(8,128)S(1)}, f32[2,128,128]{2,1,0:T(8,128)S(1)}, u32[]{:S(2)}, u32[]{:S(2)}) collective-permute-start(f32[2,128,128]{2,1,0:T(8,128)S(1)} %convolution_subtract_fusion.2), channel_id=1, source_target_pairs={{0,4},{4,8},{8,12},{12,16},{16,20},{20,24},{24,28},{1,5},{5,9},{9,... | collective-permute-start | bytes 393224 | tf_op jit(solution)/shard_map/ppermute | solution.py:16
  76.6 7.7 %collective-permute-start.3 = (bf16[2,128,128]{2,1,0:T(8,128)(2,1)S(1)}, bf16[2,128,128]{2,1,0:T(8,128)(2,1)S(1)}, u32[]{:S(2)}, u32[]{:S(2)}) collective-permute-start(bf16[2,128,128]{2,1,0:T(8,128)(2,1)S(1)} %collective-permute-done), channel_id=1, source_target_pairs={{0,4},{4,8},{8,12},{12,16},{16,20},{20,24},{24,28},{1,5},{5,9},{9,... | collective-permute-start | bytes 196616 | tf_op jit(solution)/shard_map/ppermute | solution.py:16
  81.8 12.6 %collective-permute-start.5 = (f32[2,128,128]{2,1,0:T(8,128)S(1)}, f32[2,128,128]{2,1,0:T(8,128)S(1)}, u32[]{:S(2)}, u32[]{:S(2)}) collective-permute-start(f32[2,128,128]{2,1,0:T(8,128)S(1)} %collective-permute-done.2), channel_id=1, source_target_pairs={{0,4},{4,8},{8,12},{12,16},{16,20},{20,24},{24,28},{1,5},{5,9},{9,... | collective-permute-start | bytes 393224 | tf_op jit(solution)/shard_map/ppermute | solution.py:16
  84.4 7.1 %collective-permute-start.6 = (bf16[2,128,128]{2,1,0:T(8,128)(2,1)S(1)}, bf16[2,128,128]{2,1,0:T(8,128)(2,1)S(1)}, u32[]{:S(2)}, u32[]{:S(2)}) collective-permute-start(bf16[2,128,128]{2,1,0:T(8,128)(2,1)S(1)} %collective-permute-done.3), channel_id=1, source_target_pairs={{0,4},{4,8},{8,12},{12,16},{16,20},{20,24},{24,28},{1,5},{5,9},{9,... | collective-permute-start | bytes 196616 | tf_op jit(solution)/shard_map/ppermute | solution.py:16
  91.4 11.4 %collective-permute-start.9 = (bf16[2,128,128]{2,1,0:T(8,128)(2,1)S(1)}, bf16[2,128,128]{2,1,0:T(8,128)(2,1)S(1)}, u32[]{:S(2)}, u32[]{:S(2)}) collective-permute-start(bf16[2,128,128]{2,1,0:T(8,128)(2,1)S(1)} %collective-permute-done.6), channel_id=1, source_target_pairs={{0,4},{4,8},{8,12},{12,16},{16,20},{20,24},{24,28},{1,5},{5,9},{9,... | collective-permute-start | bytes 196616 | tf_op jit(solution)/shard_map/ppermute | solution.py:16
  94.5 7.8 %collective-permute-start.8 = (f32[2,128,128]{2,1,0:T(8,128)S(1)}, f32[2,128,128]{2,1,0:T(8,128)S(1)}, u32[]{:S(2)}, u32[]{:S(2)}) collective-permute-start(f32[2,128,128]{2,1,0:T(8,128)S(1)} %collective-permute-done.5), channel_id=1, source_target_pairs={{0,4},{4,8},{8,12},{12,16},{16,20},{20,24},{24,28},{1,5},{5,9},{9,... | collective-permute-start | bytes 393224 | tf_op jit(solution)/shard_map/ppermute | solution.py:16
  105.8 7.7 %collective-permute-start.11 = (f32[2,128,128]{2,1,0:T(8,128)S(1)}, f32[2,128,128]{2,1,0:T(8,128)S(1)}, u32[]{:S(2)}, u32[]{:S(2)}) collective-permute-start(f32[2,128,128]{2,1,0:T(8,128)S(1)} %collective-permute-done.8), channel_id=1, source_target_pairs={{0,4},{4,8},{8,12},{12,16},{16,20},{20,24},{24,28},{1,5},{5,9},{9,... | collective-permute-start | bytes 393224 | tf_op jit(solution)/shard_map/ppermute | solution.py:16
Sparse Core Ops, SparseCore 0:
  11.8 22.7 reduce-scatter.1
where the time goes:
time: 122 us
  starting transfers between devices  37.5 us (31%)
  other arithmetic  22 us (18%)
  waiting for transfers between devices  19.5 us (16%)
  between operations  15.9 us (13%)
  matrix products  14.5 us (12%)
  blocking collectives  6.31 us (5%)
  local copies, waits for them, and re-layouts  6.19 us (5%)
    ppermute x12, starting transfers between devices, passed_along(): return lax.ppermute(array, axis, pairs)  37.5 us
    another operation x4, other arithmetic, transitions(): lax.linalg.triangular_solve(lower_mat, diag_beta, left_side=True, lower=T...  19.8 us
    ppermute x12, waiting for transfers between devices, passed_along(): return lax.ppermute(array, axis, pairs)  19.5 us
    unnamed x1, blocking collectives  6.31 us
    reshape x1, local copies, waits for them, and re-layouts, body(): w_proj.reshape(w_proj.shape[0], all_heads, head_dim)  2.89 us
    unnamed x20, local copies, waits for them, and re-layouts  2.87 us
  transfers between devices with their start and end apart: 13, of which 5 were waited for; matrix products, arithmetic and copies ran while one was open for 29% of the time, Pallas kernels for 0%

commit v1 on v0

v1 whole, which is shorter than its diff:
```python
import functools

import jax
import jax.numpy as jnp
from jax import lax
from jax.experimental import pallas as pl
from jax.experimental.pallas import tpu as pltpu
from jax.sharding import PartitionSpec as P

STEPS = 5
FAR = jnp.float32
PROD_PARTS = 2

very_low = -1e30
f32 = jnp.float32
bf16 = jnp.bfloat16
MESH = pl.DeviceIdType.MESH


def dot(a, b):
    return lax.dot_general(a, b, (((1,), (0,)), ((), ())), preferred_element_type=f32)


def dot_t(a, b):
    return lax.dot_general(a, b, (((1,), (1,)), ((), ())), preferred_element_type=f32)


def split(x):
    high = x.astype(bf16)
    return high, (x - high.astype(f32)).astype(bf16)


def halves(x):
    n = x.shape[1] // 2
    return x[:, :n] + x[:, n:]


def wide(x):
    return jnp.concatenate(split(x), axis=1)


def mm(a, b):
    both = wide(b)
    return halves(dot(wide(a), jnp.concatenate([both, both], axis=0)))


def mm_t(a, b):
    high, low = split(b)
    rhs = jnp.concatenate(
        [jnp.concatenate([high, high], axis=1), jnp.concatenate([low, low], axis=1)], axis=0
    )
    return halves(dot_t(wide(a), rhs))


def exact_mm_t(a, b):
    return halves(dot_t(a, jnp.concatenate(split(b), axis=0)))


def kernel(
    n_head, n_ctx,
    hid_hbm, w_hbm, b_hbm, q_hbm, k_hbm, v_hbm, reach,
    numer, totals, maxima, carried,
    hid, w, b, q, k, part, got, plog, glog, lsum, vals, bun, carry, score, qvec,
    local_sem, w_sem, part_send, part_recv, log_send, log_recv,
    val_send, val_recv, bun_send, bun_recv,
):
    me = lax.axis_index("head")
    ctx = lax.axis_index("ctx")
    parity = lax.rem(ctx, 2)
    partner = ctx + 1 - 2 * parity
    length = hid.shape[0]
    kv_heads = bun.shape[1]
    head_dim = bun.shape[3]
    groups = q.shape[1] // (kv_heads * head_dim)
    columns = kv_heads * head_dim
    scaling = head_dim ** (-0.5)
    others = sorted(range(1, n_head), key=lambda i: abs(i - n_head // 2))

    barrier = pltpu.get_barrier_semaphore()
    for i in others:
        pl.semaphore_signal(
            barrier, inc=1, device_id={"head": lax.rem(me + i, n_head)}, device_id_type=MESH
        )
    pl.semaphore_signal(barrier, inc=1, device_id={"ctx": partner}, device_id_type=MESH)
    has_next, has_last = ctx + 2 < n_ctx, ctx >= 2

    @pl.when(has_next)
    def _():
        pl.semaphore_signal(barrier, inc=1, device_id={"ctx": ctx + 2}, device_id_type=MESH)

    @pl.when(has_last)
    def _():
        pl.semaphore_signal(barrier, inc=1, device_id={"ctx": ctx - 2}, device_id_type=MESH)

    def local(src, dst, sem):
        copy = pltpu.make_async_copy(src, dst, sem)
        copy.start()
        return copy

    hid_in = local(hid_hbm, hid, local_sem.at[0])
    b_in = local(b_hbm, b, local_sem.at[1])
    w_in = []
    for i in others + [0]:
        at = pl.multiple_of(lax.rem(me + i, n_head) * columns, columns)
        w_in.append(local(w_hbm.at[:, pl.ds(at, columns)], w.at[i], w_sem.at[i]))
    v_in = local(v_hbm, vals.at[0], local_sem.at[2])
    k_in = local(k_hbm, k, local_sem.at[3])
    q_in = local(q_hbm, q, local_sem.at[4])

    row = lax.broadcasted_iota(jnp.int32, (length, length), 0)
    col = lax.broadcasted_iota(jnp.int32, (length, length), 1)
    eye = jnp.where(row == col, 1.0, 0.0).astype(f32)

    for s in range(1, STEPS):
        @pl.when(ctx < s)
        def _():
            vals[s] = jnp.zeros(vals.shape[1:], bf16)
            for h in range(kv_heads):
                bun[s, h] = jnp.zeros(bun.shape[2:], bf16)
                bun[s, h, length:2 * length] = eye.astype(bf16)

    def value_copy(kind, src, slot, to):
        return pltpu.make_async_remote_copy(
            src_ref=vals.at[src], dst_ref=vals.at[slot],
            send_sem=val_send.at[kind], recv_sem=val_recv.at[slot],
            device_id={"ctx": to}, device_id_type=MESH,
        )

    def bundle_copy(h):
        def make(kind, src, slot, to):
            return pltpu.make_async_remote_copy(
                src_ref=bun.at[src, h], dst_ref=bun.at[slot, h],
                send_sem=bun_send.at[h, kind], recv_sem=bun_recv.at[h, slot],
                device_id={"ctx": to}, device_id_type=MESH,
            )
        return make

    def stage_0(make):
        @pl.when(has_next)
        def _():
            make(0, 0, 2, ctx + 2).start()

        @pl.when(parity == 0)
        def _():
            make(1, 0, 1, partner).start()

    def stage_1(make):
        @pl.when(has_last)
        def _():
            make(0, 0, 2, partner).wait_recv()

        @pl.when(jnp.logical_and(has_last, has_next))
        def _():
            make(2, 2, 4, ctx + 2).start()

        @pl.when(jnp.logical_and(has_last, parity == 0))
        def _():
            make(3, 2, 3, partner).start()

        @pl.when(jnp.logical_and(has_last, parity == 1))
        def _():
            make(1, 2, 1, partner).start()

    def stage_2(make):
        @pl.when(ctx >= 4)
        def _():
            make(2, 0, 4, partner).wait_recv()

        @pl.when(jnp.logical_and(ctx >= 4, parity == 1))
        def _():
            make(3, 4, 3, partner).start()

    def stage_end(make):
        @pl.when(has_next)
        def _():
            make(0, 0, 2, partner).wait_send()

        @pl.when(ctx >= 2 * parity)
        def _():
            make(1, 0, 1, partner).wait_send()

        @pl.when(jnp.logical_and(has_last, has_next))
        def _():
            make(2, 0, 4, partner).wait_send()

        @pl.when(ctx >= 2 + 2 * parity)
        def _():
            make(3, 0, 3, partner).wait_send()

    def arrive(make, slot):
        @pl.when(ctx >= slot)
        def _():
            make(0, 0, slot, partner).wait_recv()

    hid_in.wait()
    b_in.wait()
    x = hid[...]
    plog[...] = lax.dot_general(
        b[...], x, (((0,), (1,)), ((), ())), preferred_element_type=f32
    )

    def part_copies(i):
        to = {"head": lax.rem(me + i, n_head)}
        return (
            pltpu.make_async_remote_copy(
                src_ref=part.at[i], dst_ref=got.at[i],
                send_sem=part_send.at[i], recv_sem=part_recv.at[i],
                device_id=to, device_id_type=MESH,
            ),
            pltpu.make_async_remote_copy(
                src_ref=plog, dst_ref=glog.at[i],
                send_sem=log_send.at[i], recv_sem=log_recv.at[i],
                device_id=to, device_id_type=MESH,
            ),
        )

    raw = None
    for n, i in enumerate(others + [0]):
        w_in[n].wait()
        term = dot(x, w[i])
        if i == 0:
            raw = term
        else:
            part[i] = term.astype(part.dtype)
            if n == 0:
                pl.semaphore_wait(
                    barrier,
                    n_head + has_next.astype(jnp.int32) + has_last.astype(jnp.int32),
                )
            for copy in part_copies(i):
                copy.start()
    v_in.wait()
    stage_0(value_copy)
    k_in.wait()
    q_in.wait()
    logit = plog[...]
    for i in others:
        for copy in part_copies(i):
            copy.wait_recv()
        raw = raw + got[i].astype(f32)
        logit = logit + glog[i]
    lsum[...] = 2.0 / (1.0 + jnp.exp(-logit))
    stage_1(value_copy)

    vec, unit, wanted, beta = [], [], [], []
    for h in range(kv_heads):
        r = raw[:, h * head_dim:(h + 1) * head_dim]
        vec.append(r * lax.rsqrt(jnp.sum(r * r, axis=-1, keepdims=True) + 1e-06))
        beta_row = lsum[pl.ds(me * kv_heads + h, 1), :]
        wide_beta = jnp.broadcast_to(beta_row, (length, length))
        beta.append(wide_beta.T)
        upper = jnp.where(row < col, mm_t(vec[h], vec[h]) * wide_beta, 0.0)
        wanted.append(upper)

    def level(size):
        return (row // (2 * size) == col // (2 * size)) & (row // size < col // size)

    unit = [eye - jnp.where(level(1), a, 0.0) for a in wanted]
    size = 2
    while size < length:
        mask = level(size)
        half = [mm(u, jnp.where(mask, a, 0.0)) for u, a in zip(unit, wanted)]
        unit = [u - mm(t, u) for u, t in zip(unit, half)]
        size *= 2

    key_low = []
    for h in range(kv_heads):
        key = k[:, h * head_dim:(h + 1) * head_dim]
        lower = jnp.where(row > col, exact_mm_t(key, vec[h]), 0.0)
        key_low.append(lower)
        y = beta[h] * mm(unit[h], vec[h])
        moved = key.astype(f32) - mm(lower, y)
        prod = eye - mm(vec[h].T, y)
        bun[0, h, 0:length] = moved.astype(bf16)
        high, low = split(prod)
        bun[0, h, length:2 * length] = high
        if PROD_PARTS == 2:
            bun[0, h, 2 * length:3 * length] = low
    for h in range(kv_heads):
        stage_0(bundle_copy(h))
    stage_2(value_copy)

    causal = jnp.concatenate([row >= col] * groups, axis=0)
    for h in range(kv_heads):
        key = k[:, h * head_dim:(h + 1) * head_dim]
        query = jnp.concatenate(
            [
                q[:, (h * groups + g) * head_dim:(h * groups + g + 1) * head_dim]
                for g in range(groups)
            ],
            axis=0,
        )
        tri = (beta[h] * unit[h]).T
        z = mm(tri, vec[h])
        mix = mm(tri, key_low[h].T)
        z_high, z_low = split(z)
        mix_high, mix_low = split(mix)
        top = jnp.concatenate([z_high, mix_high], axis=1)
        query_vec = jnp.where(causal, exact_mm_t(query, vec[h]), 0.0)
        vec_high, vec_low = split(query_vec)
        moved = dot(
            jnp.concatenate([vec_high, vec_low], axis=1), jnp.concatenate([top, top], axis=0)
        ) + dot(vec_high, jnp.concatenate([z_low, mix_low], axis=1))
        carry[h] = query.astype(f32) - moved[:, :head_dim]
        own = (dot_t(query, key) - moved[:, head_dim:]) * scaling
        score[h, 0] = jnp.where(causal, own, very_low)
        stage_1(bundle_copy(h))

    reach_now = reach[0]
    for s in range(1, STEPS):
        if s == 1:
            for h in range(kv_heads):
                arrive(bundle_copy(h), 1)
        live = jnp.logical_and(s < reach_now, ctx >= s)
        if s == 3:
            for h in range(kv_heads):
                arrive(bundle_copy(h), 3)
        for h in range(kv_heads):
            now_high, now_low = split(carry[h])
            moved = bun[s, h, 0:length]
            got_score = dot_t(now_high, moved) * scaling
            score[h, s] = jnp.where(live, got_score, very_low)
            high = bun[s, h, length:2 * length]
            now = jnp.concatenate([now_high, now_low], axis=1)
            rhs = jnp.concatenate([high, high], axis=1)
            if PROD_PARTS == 2:
                low = bun[s, h, 2 * length:3 * length]
                rhs = jnp.concatenate([rhs, jnp.concatenate([low, low], axis=1)], axis=0)
                carry[h] = halves(dot_t(now, rhs))
            else:
                carry[h] = dot_t(now, rhs)
        if s == 1:
            for h in range(kv_heads):
                stage_2(bundle_copy(h))

    arrive(value_copy, 1)
    arrive(value_copy, 3)
    lane = lax.broadcasted_iota(jnp.int32, (length, length), 1)
    stats = jnp.zeros((length, length), f32)
    n_q = kv_heads * groups
    for h in range(kv_heads):
        top = score[h, 0]
        for s in range(1, STEPS):
            top = jnp.maximum(top, score[h, s])
        top = jnp.max(top, axis=-1, keepdims=True)
        total, acc = None, None
        for s in range(STEPS):
            probs = jnp.exp(score[h, s] - top)
            value = vals[s, :, h * head_dim:(h + 1) * head_dim]
            here = dot(probs.astype(bf16), value)
            total = probs if total is None else total + probs
            acc = here if acc is None else acc + here
        total = jnp.sum(total, axis=-1, keepdims=True)
        for g in range(groups):
            rows = slice(g * length, (g + 1) * length)
            at = h * groups + g
            cols = slice(at * head_dim, (at + 1) * head_dim)
            numer[:, cols] = acc[rows]
            carried[:, cols] = carry[h, rows].astype(bf16)
            stats = jnp.where(lane == at, top[rows], stats)
            stats = jnp.where(lane == n_q + at, total[rows], stats)
    stats = stats.T
    maxima[...] = stats[:n_q]
    totals[...] = stats[n_q:2 * n_q]

    for i in others:
        for copy in part_copies(i):
            copy.wait_send()
    stage_end(value_copy)
    for h in range(kv_heads):
        stage_end(bundle_copy(h))


def solution(mesh):
    n_head, n_ctx = mesh.shape["head"], mesh.shape["ctx"]

    def body(hidden, w_proj, b_proj, queries, keys, values, reach):
        length, depth = hidden.shape
        all_heads = b_proj.shape[1]
        head_dim = w_proj.shape[1] // all_heads
        kv_heads = all_heads // n_head
        columns = kv_heads * head_dim
        n_q = queries.shape[1] // head_dim
        rows = n_q // kv_heads * length
        any_space = pl.BlockSpec(memory_space=pl.ANY)
        vmem = pl.BlockSpec(memory_space=pltpu.VMEM)
        dma = pltpu.SemaphoreType.DMA
        return pl.pallas_call(
            functools.partial(kernel, n_head, n_ctx),
            out_shape=(
                jax.ShapeDtypeStruct(queries.shape, f32),
                jax.ShapeDtypeStruct((n_q, length), f32),
                jax.ShapeDtypeStruct((n_q, length), f32),
                jax.ShapeDtypeStruct(queries.shape, bf16),
            ),
            in_specs=[any_space] * 6 + [pl.BlockSpec(memory_space=pltpu.SMEM)],
            out_specs=(vmem, vmem, vmem, vmem),
            scratch_shapes=[
                pltpu.VMEM((length, depth), bf16),
                pltpu.VMEM((n_head, depth, columns), bf16),
                pltpu.VMEM((depth, all_heads), bf16),
                pltpu.VMEM(queries.shape, bf16),
                pltpu.VMEM(keys.shape, bf16),
                pltpu.VMEM((n_head, length, columns), FAR),
                pltpu.VMEM((n_head, length, columns), FAR),
                pltpu.VMEM((all_heads, length), f32),
                pltpu.VMEM((n_head, all_heads, length), f32),
                pltpu.VMEM((all_heads, length), f32),
                pltpu.VMEM((STEPS, length, columns), bf16),
                pltpu.VMEM((STEPS, kv_heads, (1 + PROD_PARTS) * length, head_dim), bf16),
                pltpu.VMEM((kv_heads, rows, head_dim), f32),
                pltpu.VMEM((kv_heads, STEPS, rows, length), f32),
                pltpu.VMEM((8, 128), f32),
                dma((5,)),
                dma((n_head,)),
                dma((n_head,)),
                dma((n_head,)),
                dma((n_head,)),
                dma((n_head,)),
                dma((4,)),
                dma((STEPS,)),
                dma((kv_heads, 4)),
                dma((kv_heads, STEPS)),
            ],
            compiler_params=pltpu.CompilerParams(
                collective_id=0, has_side_effects=True, vmem_limit_bytes=48 << 20
            ),
        )(hidden, w_proj, b_proj, queries, keys, values, reach)

    in_specs = (
        P("ctx", "head"),
        P("head", None),
        P("head", None),
        P("ctx", "head"),
        P("ctx", "head"),
        P("ctx", "head"),
        P("ctx"),
    )
    out_specs = (P("ctx", "head"), P("head", "ctx"), P("head", "ctx"), P("ctx", "head"))
    return jax.shard_map(body, mesh=mesh, in_specs=in_specs, out_specs=out_specs, check_vma=False)
```

time: 122 us -> 38.4 us (0.31)
  the two profiles are of different devices: /device:TPU:8 before, /device:TPU:17 now
where the time goes in v1:
time: 38.4 us; the launch traced here: 38.1 us
  Pallas kernels  28 us (73%)
  local copies, waits for them, and re-layouts  8.73 us (23%)
  between operations  1.31 us (3%)
    pallas_call x1, Pallas kernels, body(): pl.pallas_call(functools.partial(kernel, n_head, n_ctx), out_shape=(jax.S...  28 us
    unnamed x15, local copies, waits for them, and re-layouts  8.73 us

profile of v1, /device:TPU:17, one launch (start us, length us, event | category | flops | bytes accessed | tf_op | source)
XLA Modules:
  0.0 38.1 jit_solution(2610424585930758436)
XLA Ops:
  1.3 0.9 %copy.11.b_hbm = bf16[1024,8]{1,0:T(8,128)(2,1)S(1)} copy(bf16[1024,8]{0,1:T(8,128)(2,1)} %param.9) | data formatting | bytes 32768 | tf_op args[2]
  2.2 0.0 copy-start
  2.2 1.6 %copy-done = bf16[1024,1024]{1,0:T(8,128)(2,1)S(1)} copy-done((bf16[1024,1024]{1,0:T(8,128)(2,1)S(1)}, bf16[1024,1024]{1,0:T(8,128)(2,1)}, u32[]{:S(2)}) %copy-start) | copy-done | bytes 2097176
  3.8 0.0 copy-start.1
  3.8 0.9 %copy-done.1 = bf16[128,1024]{1,0:T(8,128)(2,1)S(1)} copy-done((bf16[128,1024]{1,0:T(8,128)(2,1)S(1)}, bf16[128,1024]{1,0:T(8,128)(2,1)}, u32[]{:S(2)}) %copy-start.1) | copy-done | bytes 262168
  4.7 0.0 copy-start.2
  4.7 0.9 %copy-done.2 = bf16[128,1024]{1,0:T(8,128)(2,1)S(1)} copy-done((bf16[128,1024]{1,0:T(8,128)(2,1)S(1)}, bf16[128,1024]{1,0:T(8,128)(2,1)}, u32[]{:S(2)}) %copy-start.2) | copy-done | bytes 262168
  5.7 0.0 copy-start.3
  5.7 0.8 %copy-done.3 = bf16[128,256]{1,0:T(8,128)(2,1)S(1)} copy-done((bf16[128,256]{1,0:T(8,128)(2,1)S(1)}, bf16[128,256]{1,0:T(8,128)(2,1)}, u32[]{:S(2)}) %copy-start.3) | copy-done | bytes 65560
  6.5 0.0 copy-start.4
  6.5 0.8 %copy-done.4 = bf16[128,256]{1,0:T(8,128)(2,1)S(1)} copy-done((bf16[128,256]{1,0:T(8,128)(2,1)S(1)}, bf16[128,256]{1,0:T(8,128)(2,1)}, u32[]{:S(2)}) %copy-start.4) | copy-done | bytes 65560
  7.3 28.0 %shard_map.102 = (f32[128,1024]{1,0:T(8,128)S(1)}, f32[8,128]{1,0:T(8,128)S(1)}, f32[8,128]{1,0:T(8,128)S(1)}, bf16[128,1024]{1,0:T(8,128)(2,1)S(1)}) custom-call(bf16[128,1024]{1,0:T(8,128)(2,1)S(1)} %copy-done.1, bf16[1024,1024]{1,0:T(8,128)(2,1)S(1)} %copy-done, bf16[1024,8]{1,0:T(8,128)(2,1)S(1)} %copy.11.b_hbm, bf16[128,1024]{1,0:T(8,128)(2,1)S(1)} %copy-done.2, ...), custom_call_target="tpu_custom_call" | custom-call | tf_op jit(solution)/shard_map/pallas_call | solution.py:388
  35.4 0.8 %copy.17 = f32[128,1024]{1,0:T(8,128)} copy(f32[128,1024]{1,0:T(8,128)S(1)} %get-tuple-element.8) | data formatting | bytes 1048576
  36.2 0.6 %copy.18 = f32[8,128]{1,0:T(8,128)} copy(f32[8,128]{1,0:T(8,128)S(1)} %get-tuple-element.9) | data formatting | bytes 8192
  36.8 0.6 %copy.19 = f32[8,128]{1,0:T(8,128)} copy(f32[8,128]{1,0:T(8,128)S(1)} %get-tuple-element.10) | data formatting | bytes 8192
  37.4 0.7 %copy.20 = bf16[128,1024]{1,0:T(8,128)(2,1)} copy(bf16[128,1024]{1,0:T(8,128)(2,1)S(1)} %get-tuple-element.11) | data formatting | bytes 524288
Async XLA Ops:
  2.2 1.6 %copy-start = (bf16[1024,1024]{1,0:T(8,128)(2,1)S(1)}, bf16[1024,1024]{1,0:T(8,128)(2,1)}, u32[]{:S(2)}) copy-start(bf16[1024,1024]{1,0:T(8,128)(2,1)} %w_hbm.1) | copy-start | bytes 6291460
  3.8 0.9 %copy-start.1 = (bf16[128,1024]{1,0:T(8,128)(2,1)S(1)}, bf16[128,1024]{1,0:T(8,128)(2,1)}, u32[]{:S(2)}) copy-start(bf16[128,1024]{1,0:T(8,128)(2,1)} %hid_hbm.1) | copy-start | bytes 786436
  4.7 0.9 %copy-start.2 = (bf16[128,1024]{1,0:T(8,128)(2,1)S(1)}, bf16[128,1024]{1,0:T(8,128)(2,1)}, u32[]{:S(2)}) copy-start(bf16[128,1024]{1,0:T(8,128)(2,1)} %q_hbm.1) | copy-start | bytes 786436
  5.7 0.8 %copy-start.3 = (bf16[128,256]{1,0:T(8,128)(2,1)S(1)}, bf16[128,256]{1,0:T(8,128)(2,1)}, u32[]{:S(2)}) copy-start(bf16[128,256]{1,0:T(8,128)(2,1)} %k_hbm.1) | copy-start | bytes 196612
  6.5 0.8 %copy-start.4 = (bf16[128,256]{1,0:T(8,128)(2,1)S(1)}, bf16[128,256]{1,0:T(8,128)(2,1)}, u32[]{:S(2)}) copy-start(bf16[128,256]{1,0:T(8,128)(2,1)} %v_hbm.1) | copy-start | bytes 196612
